TPU v7x, 32 devices: a whole 2x2x4 slice. The times are simulated.
32 devices in a mesh: seq: 16 (over z, x, core), tp: 2 (over y).
Axes of the slice: x: 2, y: 2, z: 4, core: 2. Of those that a mesh axis runs over, the one named last changes fastest.
Arguments:
- hidden_in: bfloat16 [2048, 4096], P('seq', 'tp'), may hold values from -64 to 64
- span_order: int32 [16], replicated, may hold values from 0 to 15, each once
- norm_gain: bfloat16 [4096], P('tp'), may hold values from 0.099609375 to 1.8984375
- w_query: bfloat16 [4096, 4096], P('seq', 'tp'), may hold values from -0.09375 to 0.09375
- bias_query: bfloat16 [4096], P('tp'), may hold values from -14 to 14
- key_value_weight: bfloat16 [4096, 2, 1024], P('seq', None, 'tp'), may hold values from -0.09375 to 0.09375
- bias_kv: bfloat16 [2, 1024], P(None, 'tp'), may hold values from -14 to 14
- w_out: bfloat16 [4096, 4096], P('tp', 'seq'), may hold values from -0.09375 to 0.09375
- post_gain: bfloat16 [4096], P('tp'), may hold values from 0.099609375 to 1.8984375
Outputs:
- attn_out: bfloat16 [2048, 4096], P('seq', 'tp')
- normed: bfloat16 [2048, 4096], P('seq', 'tp')
Inputs may be any that keep to these rules, and one draw needn't show every extreme that they name: Each span number appears once; row r of hidden_in belongs to span span_order[r // 128].
All inputs are finite; a program needn't handle non-finite values.
Results may differ from a plain program's by a relative error of at most 0.014.
Values may be sent and summed in bfloat16 or wider, within the bound.
A program may use at most 128 MiB of HBM per device.

v0:
```python
import math
import jax
import jax.numpy as jnp
from jax import lax
from jax.sharding import PartitionSpec as P

MODEL_WIDTH = 4096
HEAD_SIZE = 128
GROUP = 4
eps = 1e-06
rope_base = 1000000.0


def apply_rotary(field, token_positions):
    half = field.shape[-1] // 2
    inverse = jnp.exp(-math.log(rope_base) * jnp.arange(half, dtype=jnp.float32) / half)
    angles = token_positions.astype(jnp.float32)[:, None] * inverse[None, :]
    cosine = jnp.cos(angles)[:, None, :]
    sine = jnp.sin(angles)[:, None, :]
    first = field[..., :half]
    second = field[..., half:]
    return jnp.concatenate(
        [first * cosine - second * sine, second * cosine + first * sine], axis=-1
    )


def span_lookup(order, devices):
    table_ids = jnp.arange(order.shape[0], dtype=jnp.int32)
    return jnp.sum(jnp.where(devices[:, None] == table_ids[None, :], order[None, :], 0), axis=1)


def per_device(
    hidden_in,
    span_order,
    norm_gain,
    w_query,
    bias_query,
    key_value_weight,
    bias_kv,
    w_out,
    post_gain,
):
    tok_rows = hidden_in.shape[0]
    seq_index = lax.axis_index("seq")
    own_span = span_lookup(span_order, jnp.full((1,), seq_index, jnp.int32))[0]
    token_positions = own_span * tok_rows + jnp.arange(tok_rows, dtype=jnp.int32)
    local = hidden_in.astype(jnp.float32)
    raw_rows, gains = (
        lax.all_gather(hidden_in, "tp", axis=1, tiled=True),
        lax.all_gather(norm_gain[None, :], "tp", axis=1, tiled=True),
    )
    full_rows = raw_rows.astype(jnp.float32)
    meansq = jnp.mean(full_rows * full_rows, axis=1, keepdims=True)
    normed_in = (full_rows * lax.rsqrt(meansq + eps) * gains.astype(jnp.float32)).astype(
        jnp.bfloat16
    )
    columns = normed_in
    query_proj = jnp.dot(
        columns,
        lax.all_gather(w_query, "seq", axis=0, tiled=True),
        preferred_element_type=jnp.float32,
    )
    columns = normed_in
    pair_proj = jnp.einsum(
        "tr,rkc->tkc",
        columns,
        lax.all_gather(key_value_weight, "seq", axis=0, tiled=True),
        preferred_element_type=jnp.float32,
    )
    query_heads = w_query.shape[1] // HEAD_SIZE
    kv_heads = key_value_weight.shape[2] // HEAD_SIZE
    query_proj = query_proj + bias_query.astype(jnp.float32)[None, :]
    queries = apply_rotary(
        query_proj.reshape(tok_rows, query_heads, HEAD_SIZE), token_positions
    ).astype(jnp.bfloat16)
    pair_proj = pair_proj + bias_kv.astype(jnp.float32)[None, :, :]
    rotated_keys = apply_rotary(
        pair_proj[:, 0, :].reshape(tok_rows, kv_heads, HEAD_SIZE), token_positions
    )
    rotated_keys = rotated_keys.astype(jnp.bfloat16).reshape(tok_rows, kv_heads * HEAD_SIZE)
    value_rows = pair_proj[:, 1, :].astype(jnp.bfloat16)
    grouped = (
        queries.reshape(tok_rows, kv_heads, GROUP, HEAD_SIZE)
        .transpose(1, 2, 0, 3)
        .reshape(kv_heads, GROUP * tok_rows, HEAD_SIZE)
    )
    query_pos = jnp.tile(token_positions, GROUP)
    last_query = jnp.max(token_positions)
    scale = 1.0 / math.sqrt(HEAD_SIZE)
    start_state = (
        jnp.full((kv_heads, GROUP * tok_rows), -1e30, jnp.float32),
        jnp.zeros((kv_heads, GROUP * tok_rows), jnp.float32),
        jnp.zeros((kv_heads, GROUP * tok_rows, HEAD_SIZE), jnp.float32),
    )
    key_piece = lax.all_gather(rotated_keys, "seq", axis=0, tiled=True)
    value_piece = lax.all_gather(value_rows, "seq", axis=0, tiled=True)
    count = key_piece.shape[0]
    block = math.gcd(count, 1536)

    def visit(step, state):
        first = step * block
        key_block = lax.dynamic_slice_in_dim(key_piece, first, block, 0).reshape(
            block, kv_heads, HEAD_SIZE
        )
        value_block = lax.dynamic_slice_in_dim(value_piece, first, block, 0).reshape(
            block, kv_heads, HEAD_SIZE
        )
        row_ids = first + jnp.arange(block, dtype=jnp.int32)
        key_pos = span_lookup(span_order, row_ids // tok_rows) * tok_rows + row_ids % tok_rows

        def update(current):
            maxima, totals, sums = current
            scores = (
                jnp.einsum("kqd,nkd->kqn", grouped, key_block, preferred_element_type=jnp.float32)
                * scale
            )
            allowed = (key_pos[None, :] <= query_pos[:, None])[None, :, :]
            scores = jnp.where(allowed, scores, -1e30)
            fresh = jnp.maximum(maxima, jnp.max(scores, axis=2))
            weights = jnp.where(allowed, jnp.exp(scores - fresh[:, :, None]), 0.0)
            factor = jnp.exp(maxima - fresh)
            totals = totals * factor + jnp.sum(weights, axis=2)
            sums = sums * factor[:, :, None] + jnp.einsum(
                "kqn,nkd->kqd",
                weights.astype(jnp.bfloat16),
                value_block,
                preferred_element_type=jnp.float32,
            )
            return (fresh, totals, sums)

        return lax.cond(jnp.min(key_pos) <= last_query, update, lambda current: current, state)

    maxima, totals, sums = lax.fori_loop(0, count // block, visit, start_state)
    attended = (sums / totals[:, :, None]).astype(jnp.bfloat16)
    attended = (
        attended.reshape(kv_heads, GROUP, tok_rows, HEAD_SIZE)
        .transpose(2, 0, 1, 3)
        .reshape(tok_rows, query_heads * HEAD_SIZE)
    )
    partial_out = jnp.dot(
        attended,
        lax.all_gather(w_out, "seq", axis=1, tiled=True),
        preferred_element_type=jnp.float32,
    )
    mixed = lax.psum_scatter(
        partial_out.astype(jnp.bfloat16), "tp", scatter_dimension=1, tiled=True
    ).astype(jnp.float32)
    attn_out = mixed.astype(jnp.bfloat16)
    stream = local + mixed
    post_sq = lax.psum(jnp.sum(stream * stream, axis=1), "tp")
    normed = (
        stream
        * lax.rsqrt(post_sq / MODEL_WIDTH + eps)[:, None]
        * post_gain.astype(jnp.float32)[None, :]
    ).astype(jnp.bfloat16)
    return (attn_out, normed)


def solution(mesh):
    placed = (
        P("seq", "tp"),
        P(),
        P("tp"),
        P("seq", "tp"),
        P("tp"),
        P("seq", None, "tp"),
        P(None, "tp"),
        P("tp", "seq"),
        P("tp"),
    )
    return jax.shard_map(
        per_device,
        mesh=mesh,
        in_specs=placed,
        out_specs=(P("seq", "tp"), P("seq", "tp")),
        check_vma=False,
    )
```

profile of v0, /device:TPU:0, one launch (start us, length us, event | category | flops | bytes accessed | tf_op | source)
XLA Modules:
  0.0 499.7 jit_solution(17849845767442077635)
XLA Ops:
  7.9 1.9 copy.44
  9.9 5.5 %all-gather = bf16[4096]{0:T(1024)(128)(2,1)S(1)} all-gather(bf16[2048]{0:T(1024)(128)(2,1)} %param.15), channel_id=2, replica_groups=mesh['seq'=16,'tp'=2] {'tp'}, dimensions={0}, use_global_device_ids=true | all-gather | bytes 12288 | tf_op jit(solution)/shard_map/all_gather | solution.py:50
  16.1 17.4 %all-gather.9.cloned.1.call-done = bf16[128,4096]{1,0:T(8,128)(2,1)} async-done(((bf16[128,2048]{1,0:T(8,128)(2,1)}), bf16[128,4096]{1,0:T(8,128)(2,1)}) %all-gather.9.cloned.1.call-update) | async-done | bytes 1048592 | tf_op jit(solution)/shard_map/all_gather | solution.py:49
  35.1 75.6 %all-gather.11.cloned.1.call-done = bf16[4096,2,512]{2,0,1:T(8,128)(2,1)} async-done(((bf16[256,2,512]{2,0,1:T(8,128)(2,1)}), bf16[4096,2,512]{2,0,1:T(8,128)(2,1)}) %all-gather.11.cloned.1.call-update) | async-done | bytes 8388624 | tf_op jit(solution)/shard_map/all_gather | solution.py:67
  110.7 5.0 %convolution_add_fusion.1 = f32[128,2,512]{2,0,1:T(8,128)S(1)} fusion(bf16[4096,2,512]{2,0,1:T(8,128)(2,1)} %all-gather.11.cloned.1.call-done, bf16[128,4096]{1,0:T(8,128)(2,1)} %all-gather.9.cloned.1.call-done, f32[4096]{0:T(1024)S(1)} %mul.210, f32[128]{0:T(128)S(1)} %add_rsqrt_fusion.1, f32[2,512]{1,0:T(2,128)S(1)} %convert_element_type.69), kind=kOutput, calls=%fused_computation.39 | convolution fusion | flops 1075970048 | bytes 9982464 | tf_op jit(solution)/shard_map/tr,rkc->tkc/dot_general | solution.py:64
  121.5 35.1 %all-gather.19.cloned.1.call-done = bf16[2048,1,512]{2,0,1:T(8,128)(2,1)} async-done(((bf16[128,1,512]{2,0,1:T(8,128)(2,1)}), bf16[2048,1,512]{2,0,1:T(8,128)(2,1)}) %all-gather.19.cloned.1.call-update) | async-done | bytes 2097168 | tf_op jit(solution)/shard_map/all_gather | solution.py:96
  156.6 2.9 copy.48
  159.5 124.3 %all-gather.15.cloned.1.call-done = bf16[4096,2048]{1,0:T(8,128)(2,1)} async-done(((bf16[256,2048]{1,0:T(8,128)(2,1)}), bf16[4096,2048]{1,0:T(8,128)(2,1)}) %all-gather.15.cloned.1.call-update) | async-done | bytes 16777232 | tf_op jit(solution)/shard_map/all_gather | solution.py:60
  283.8 8.2 %fusion.21 = f32[16,8,16,128]{3,1,2,0:T(8,128)S(1)} fusion(bf16[4096,2048]{1,0:T(8,128)(2,1)} %all-gather.15.cloned.1.call-done, f32[2048]{0:T(1024)S(1)} %convert_element_type.72, bf16[128,4096]{1,0:T(8,128)(2,1)S(1)} %copy-done, f32[4096]{0:T(1024)S(1)} %mul.210, f32[128]{0:T(128)S(1)} %add_rsqrt_fusion.1), kind=kOutput, calls=%fused_computation.38 | convolution fusion | flops 2149842944 | bytes 18899456 | tf_op jit(solution)/shard_map/dot_general | solution.py:58
  293.3 32.3 %all-gather.13.cloned.1.call-done = bf16[2048,512]{0,1:T(8,128)(2,1)} async-done(((bf16[128,512]{0,1:T(8,128)(2,1)}), bf16[2048,512]{0,1:T(8,128)(2,1)}) %all-gather.13.cloned.1.call-update) | async-done | bytes 2097168 | tf_op jit(solution)/shard_map/all_gather | solution.py:95
  326.7 33.3 %while.20 = (s32[]{:T(128)}, f32[4,512]{1,0:T(4,128)S(1)}, f32[4,512]{1,0:T(4,128)S(1)}, f32[4,512,128]{2,1,0:T(8,128)}, s32[16]{0:T(128)S(1)}, /*index=5*/s32[]...) while((s32[]{:T(128)}, f32[4,512]{1,0:T(4,128)S(1)}, ...), condition=%wide.region_10.11_spmd.clone, body=%wide.region_3.10_spmd.clone.sunk | while | flops 551332864 | bytes 27935672 | solution.py:133
  328.7 6.3 %conditional.3 = ((f32[4,512]{1,0:T(4,128)S(1)}, f32[4,512]{1,0:T(4,128)S(1)}, f32[4,512,128]{2,1,0:T(8,128)})) conditional(s32[]{:T(128)} %convert_element_type.117, (f32[4,512]{1,0:T(4,128)S(1)}, f32[4,512]{1,0:T(4,128)S(1)}, f32[4,512,128]{2,1,0:T(8,128)}) %tuple.77, (s32[512]{0:T(512)S(1)}, s32[128]{0:T(128)S(1)}, s32[]{:T(128)}, ...), branch_computations={%region_6.6_spmd, %region_7.9_spmd} | conditional | flops 551292928 | bytes 27925118 | solution.py:131
  332.2 1.8 fusion.8
  337.0 6.3 %conditional.3 = ((f32[4,512]{1,0:T(4,128)S(1)}, f32[4,512]{1,0:T(4,128)S(1)}, f32[4,512,128]{2,1,0:T(8,128)})) conditional(s32[]{:T(128)} %convert_element_type.117, (f32[4,512]{1,0:T(4,128)S(1)}, f32[4,512]{1,0:T(4,128)S(1)}, f32[4,512,128]{2,1,0:T(8,128)}) %tuple.77, (s32[512]{0:T(512)S(1)}, s32[128]{0:T(128)S(1)}, s32[]{:T(128)}, ...), branch_computations={%region_6.6_spmd, %region_7.9_spmd} | conditional | flops 551292928 | bytes 27925118 | solution.py:131
  340.6 1.8 fusion.8
  345.4 6.3 %conditional.3 = ((f32[4,512]{1,0:T(4,128)S(1)}, f32[4,512]{1,0:T(4,128)S(1)}, f32[4,512,128]{2,1,0:T(8,128)})) conditional(s32[]{:T(128)} %convert_element_type.117, (f32[4,512]{1,0:T(4,128)S(1)}, f32[4,512]{1,0:T(4,128)S(1)}, f32[4,512,128]{2,1,0:T(8,128)}) %tuple.77, (s32[512]{0:T(512)S(1)}, s32[128]{0:T(128)S(1)}, s32[]{:T(128)}, ...), branch_computations={%region_6.6_spmd, %region_7.9_spmd} | conditional | flops 551292928 | bytes 27925118 | solution.py:131
  348.9 1.8 fusion.8
  353.7 6.3 %conditional.3 = ((f32[4,512]{1,0:T(4,128)S(1)}, f32[4,512]{1,0:T(4,128)S(1)}, f32[4,512,128]{2,1,0:T(8,128)})) conditional(s32[]{:T(128)} %convert_element_type.117, (f32[4,512]{1,0:T(4,128)S(1)}, f32[4,512]{1,0:T(4,128)S(1)}, f32[4,512,128]{2,1,0:T(8,128)}) %tuple.77, (s32[512]{0:T(512)S(1)}, s32[128]{0:T(128)S(1)}, s32[]{:T(128)}, ...), branch_computations={%region_6.6_spmd, %region_7.9_spmd} | conditional | flops 551292928 | bytes 27925118 | solution.py:131
  357.2 1.8 fusion.8
  361.8 94.8 %all-gather.17.cloned.1.call-done = bf16[2048,4096]{1,0:T(8,128)(2,1)} async-done(((bf16[2048,256]{1,0:T(8,128)(2,1)}), bf16[2048,4096]{1,0:T(8,128)(2,1)}) %all-gather.17.cloned.1.call-update) | async-done | bytes 16777232 | tf_op jit(solution)/shard_map/all_gather | solution.py:142
  456.6 9.2 %convolution_convert_fusion = bf16[128,4096]{1,0:T(8,128)(2,1)} fusion(bf16[128,2048]{0,1:T(8,128)(2,1)S(1)} %bitcast.47, bf16[2048,4096]{1,0:T(8,128)(2,1)} %all-gather.17.cloned.1.call-done), kind=kOutput, calls=%fused_computation.31 | convolution fusion | flops 2148007936 | bytes 18350080 | tf_op jit(solution)/shard_map/dot_general | solution.py:140
  465.9 18.7 %reduce-scatter.2.cloned.1.call-done = bf16[128,2048]{1,0:T(8,128)(2,1)} async-done(((bf16[128,4096]{1,0:T(8,128)(2,1)}), bf16[128,2048]{1,0:T(8,128)(2,1)}) %reduce-scatter.2.cloned.1.call-update) | async-done | bytes 524304 | tf_op jit(solution)/shard_map/reduce_scatter | solution.py:145
  485.9 4.9 psum.7
  490.8 2.0 multiply_convert_fusion
  (113 shorter events, 34.3 us)
Async XLA Ops:
  7.2 26.4 %all-gather.9.cloned.1.call-start = ((), (), s32[]{:S(2)}) async-start(), calls=%async_computation.1 | async-start | bytes 1572864 | tf_op jit(solution)/shard_map/all_gather | solution.py:49
  7.9 102.8 %all-gather.11.cloned.1.call-start = ((), (), s32[]{:S(2)}) async-start(), calls=%async_computation.2 | async-start | bytes 8912896 | tf_op jit(solution)/shard_map/all_gather | solution.py:67
  9.9 146.8 %all-gather.19.cloned.1.call-start = ((), (), s32[]{:S(2)}) async-start(), calls=%async_computation.7 | async-start | bytes 2228224 | tf_op jit(solution)/shard_map/all_gather | solution.py:96
  35.1 81.9 %copy-start.4 = (s32[16]{0:T(128)S(1)}, s32[16]{0:T(128)}, u32[]{:S(2)}) copy-start(s32[16]{0:T(128)} %param.14) | copy-start | bytes 196
  115.7 5.2 %copy-start.5 = (bf16[2048]{0:T(1024)(128)(2,1)S(1)}, bf16[2048]{0:T(1024)(128)(2,1)}, u32[]{:S(2)}) copy-start(bf16[2048]{0:T(1024)(128)(2,1)} %param.17) | copy-start | bytes 12292
  116.4 167.4 %all-gather.15.cloned.1.call-start = ((), (), s32[]{:S(2)}) async-start(), calls=%async_computation.4 | async-start | bytes 17825792 | tf_op jit(solution)/shard_map/all_gather | solution.py:60
  117.0 166.8 %copy-start = (bf16[128,4096]{1,0:T(8,128)(2,1)S(1)}, bf16[128,4096]{1,0:T(8,128)(2,1)}, u32[]{:S(2)}) copy-start(bf16[128,4096]{1,0:T(8,128)(2,1)} %all-gather.9.cloned.1.call-done) | copy-start | bytes 3145732
  117.0 208.7 %all-gather.13.cloned.1.call-start = ((), (), s32[]{:S(2)}) async-start(), calls=%async_computation.3 | async-start | bytes 2228224 | tf_op jit(solution)/shard_map/all_gather | solution.py:95
  120.1 336.6 %all-gather.17.cloned.1.call-start = ((), (), s32[]{:S(2)}) async-start(), calls=%async_computation.5 | async-start | bytes 17825792 | tf_op jit(solution)/shard_map/all_gather | solution.py:142
  120.7 363.9 %reduce-scatter.2.cloned.1.call-start = ((), (), s32[]{:S(2)}) async-start(), calls=%async_computation.6 | async-start | bytes 1572864 | tf_op jit(solution)/shard_map/reduce_scatter | solution.py:145
  330.1 2.1 copy-start.2
  334.0 1.0 copy-start.3
  338.4 2.1 copy-start.2
  342.4 1.0 copy-start.3
  346.8 2.1 copy-start.2
  350.7 1.0 copy-start.3
  355.1 2.1 copy-start.2
  359.0 1.0 copy-start.3
  456.6 9.2 %copy-start.6 = (bf16[2048]{0:T(1024)(128)(2,1)S(1)}, bf16[2048]{0:T(1024)(128)(2,1)}, u32[]{:S(2)}) copy-start(bf16[2048]{0:T(1024)(128)(2,1)} %param.21) | copy-start | bytes 12292
  456.6 27.9 %copy-start.1 = (bf16[128,2048]{1,0:T(8,128)(2,1)S(1)}, bf16[128,2048]{1,0:T(8,128)(2,1)}, u32[]{:S(2)}) copy-start(bf16[128,2048]{1,0:T(8,128)(2,1)} %param.13) | copy-start | bytes 1572868
Sparse Core Ops, SparseCore 0:
  9.5 23.9 all-gather.8
  36.3 74.2 all-gather.10
  116.5 40.0 all-gather.18
  158.6 125.1 all-gather.14
  286.4 39.2 all-gather.12
  327.7 128.9 all-gather.16
  466.0 18.5 reduce-scatter.1
where the time goes:
time: 500 us
  waiting for transfers between devices  400 us (80%)
  matrix products  33.6 us (7%)
  other arithmetic  18.1 us (4%)
  local copies, waits for them, and re-layouts  16.7 us (3%)
  between operations  15 us (3%)
  blocking collectives  10.4 us (2%)
  loops' own time  5.46 us (1%)
    all_gather x1, waiting for transfers between devices, per_device(): lax.all_gather(w_query, 'seq', axis=0, tiled=True)  124 us
    all_gather x1, waiting for transfers between devices, per_device(): lax.all_gather(w_out, 'seq', axis=1, tiled=True)  94.8 us
    all_gather x1, waiting for transfers between devices, per_device(): lax.all_gather(key_value_weight, 'seq', axis=0, tiled=True)  75.6 us
    all_gather x1, waiting for transfers between devices, per_device(): value_piece = lax.all_gather(value_rows, 'seq', axis=0, tiled=True)  35.1 us
    all_gather x1, waiting for transfers between devices, per_device(): key_piece = lax.all_gather(rotated_keys, 'seq', axis=0, tiled=True)  32.3 us
    reduce_scatter x1, waiting for transfers between devices, per_device(): lax.psum_scatter(partial_out.astype(jnp.bfloat16), 'tp', scatter_dimensio...  18.7 us
    all_gather x1, waiting for transfers between devices, per_device(): lax.all_gather(hidden_in, 'tp', axis=1, tiled=True)  17.4 us
  transfers between devices with their start and end apart: 7, of which 7 were waited for; matrix products, arithmetic and copies ran while one was open for 9% of the time, Pallas kernels for 0%

commit v1 on v0

--- a/solution.py
+++ b/solution.py
@@ -3,6 +3,7 @@
 import jax.numpy as jnp
 from jax import lax
 from jax.sharding import PartitionSpec as P
+from jax.lax import all_gather
 
 MODEL_WIDTH = 4096
 HEAD_SIZE = 128
@@ -92,8 +93,14 @@
         jnp.zeros((kv_heads, GROUP * tok_rows), jnp.float32),
         jnp.zeros((kv_heads, GROUP * tok_rows, HEAD_SIZE), jnp.float32),
     )
-    key_piece = lax.all_gather(rotated_keys, "seq", axis=0, tiled=True)
-    value_piece = lax.all_gather(value_rows, "seq", axis=0, tiled=True)
+    _order_boxes = lambda slab_in, arr_in, lane_axis: jnp.split(
+        all_gather(
+            jnp.concatenate([slab_in, arr_in], axis=1), axis_name=lane_axis, axis=0, tiled=True
+        ),
+        [slab_in.shape[1]],
+        axis=1,
+    )
+    key_piece, value_piece = _order_boxes(rotated_keys, value_rows, "seq")
     count = key_piece.shape[0]
     block = math.gcd(count, 1536)
 

time: 500 us -> 467 us (0.934)
  waiting for transfers between devices: 400 us -> 358 us
  local copies, waits for them, and re-layouts: 16.7 us -> 23.9 us
    all_gather x2 -> x1, waiting for transfers between devices: 67.4 us -> 47 us  [per_device(): all_gather(jnp.concatenate([slab_in, arr_in], axis=1), axis_name=lane_axi...]
    all_gather x1, waiting for transfers between devices: 94.8 us -> 84.1 us  [per_device(): lax.all_gather(w_out, 'seq', axis=1, tiled=True)]
    all_gather x1, waiting for transfers between devices: 124 us -> 115 us  [per_device(): lax.all_gather(w_query, 'seq', axis=0, tiled=True)]
  transfers between devices with their start and end apart: 7 -> 6, of which waited for: 7 -> 6; matrix products, arithmetic and copies ran while one was open for 9% -> 12% of each run, Pallas kernels for 0% -> 0%
where the time goes in v1:
time: 467 us
  waiting for transfers between devices  358 us (77%)
  matrix products  33.6 us (7%)
  local copies, waits for them, and re-layouts  23.9 us (5%)
  other arithmetic  19.8 us (4%)
  between operations  14.9 us (3%)
  blocking collectives  10.4 us (2%)
  loops' own time  5.66 us (1%)
    all_gather x1, waiting for transfers between devices, per_device(): lax.all_gather(w_query, 'seq', axis=0, tiled=True)  115 us
    all_gather x1, waiting for transfers between devices, per_device(): lax.all_gather(w_out, 'seq', axis=1, tiled=True)  84.1 us
    all_gather x1, waiting for transfers between devices, per_device(): lax.all_gather(key_value_weight, 'seq', axis=0, tiled=True)  75.7 us
    all_gather x1, waiting for transfers between devices, per_device(): all_gather(jnp.concatenate([slab_in, arr_in], axis=1), axis_name=lane_axi...  47 us
    reduce_scatter x1, waiting for transfers between devices, per_device(): lax.psum_scatter(partial_out.astype(jnp.bfloat16), 'tp', scatter_dimensio...  18.7 us
    all_gather x1, waiting for transfers between devices, per_device(): lax.all_gather(hidden_in, 'tp', axis=1, tiled=True)  15.1 us
  transfers between devices with their start and end apart: 6, of which 6 were waited for; matrix products, arithmetic and copies ran while one was open for 12% of the time, Pallas kernels for 0%

profile of v1, /device:TPU:0, one launch (start us, length us, event | category | flops | bytes accessed | tf_op | source)
XLA Modules:
  0.0 466.6 jit_solution(11106249230774899603)
XLA Ops:
  7.9 1.9 copy.44
  9.9 5.5 %all-gather = bf16[4096]{0:T(1024)(128)(2,1)S(1)} all-gather(bf16[2048]{0:T(1024)(128)(2,1)} %param.15), channel_id=2, replica_groups=mesh['seq'=16,'tp'=2] {'tp'}, dimensions={0}, use_global_device_ids=true | all-gather | bytes 12288 | tf_op jit(solution)/shard_map/all_gather | solution.py:51
  18.4 15.1 %all-gather.7.cloned.1.call-done = bf16[128,4096]{1,0:T(8,128)(2,1)} async-done(((bf16[128,2048]{1,0:T(8,128)(2,1)}), bf16[128,4096]{1,0:T(8,128)(2,1)}) %all-gather.7.cloned.1.call-update) | async-done | bytes 1048592 | tf_op jit(solution)/shard_map/all_gather | solution.py:50
  35.1 75.7 %all-gather.9.cloned.1.call-done = bf16[4096,2,512]{2,0,1:T(8,128)(2,1)} async-done(((bf16[256,2,512]{2,0,1:T(8,128)(2,1)}), bf16[4096,2,512]{2,0,1:T(8,128)(2,1)}) %all-gather.9.cloned.1.call-update) | async-done | bytes 8388624 | tf_op jit(solution)/shard_map/all_gather | solution.py:68
  110.7 5.0 %convolution_add_fusion.1 = f32[128,2,512]{2,0,1:T(8,128)S(1)} fusion(bf16[4096,2,512]{2,0,1:T(8,128)(2,1)} %all-gather.9.cloned.1.call-done, bf16[128,4096]{1,0:T(8,128)(2,1)} %all-gather.7.cloned.1.call-done, f32[4096]{0:T(1024)S(1)} %mul.210, f32[128]{0:T(128)S(1)} %add_rsqrt_fusion.1, f32[2,512]{1,0:T(2,128)S(1)} %convert_element_type.69), kind=kOutput, calls=%fused_computation.39 | convolution fusion | flops 1075970048 | bytes 9982464 | tf_op jit(solution)/shard_map/tr,rkc->tkc/dot_general | solution.py:65
  119.3 47.0 %all-gather.11.cloned.1.call-done = bf16[2048,1024]{1,0:T(8,128)(2,1)} async-done(((bf16[128,1024]{1,0:T(8,128)(2,1)}), bf16[2048,1024]{1,0:T(8,128)(2,1)}) %all-gather.11.cloned.1.call-update) | async-done | bytes 4194320 | tf_op jit(solution)/shard_map/all_gather | solution.py:97
  166.3 4.4 fusion.31
  170.8 3.0 copy.47
  173.8 4.1 copy.48
  177.9 115.4 %all-gather.13.cloned.1.call-done = bf16[4096,2048]{1,0:T(8,128)(2,1)} async-done(((bf16[256,2048]{1,0:T(8,128)(2,1)}), bf16[4096,2048]{1,0:T(8,128)(2,1)}) %all-gather.13.cloned.1.call-update) | async-done | bytes 16777232 | tf_op jit(solution)/shard_map/all_gather | solution.py:61
  293.3 8.2 %fusion.21 = f32[16,8,16,128]{3,1,2,0:T(8,128)S(1)} fusion(bf16[4096,2048]{1,0:T(8,128)(2,1)} %all-gather.13.cloned.1.call-done, f32[2048]{0:T(1024)S(1)} %convert_element_type.73, bf16[128,4096]{1,0:T(8,128)(2,1)S(1)} %copy-done, f32[4096]{0:T(1024)S(1)} %mul.210, f32[128]{0:T(128)S(1)} %add_rsqrt_fusion.1), kind=kOutput, calls=%fused_computation.38 | convolution fusion | flops 2149842944 | bytes 18899456 | tf_op jit(solution)/shard_map/dot_general | solution.py:59
  303.9 33.7 %while.20 = (s32[]{:T(128)}, f32[4,512]{1,0:T(4,128)S(1)}, f32[4,512]{1,0:T(4,128)S(1)}, f32[4,512,128]{2,1,0:T(8,128)}, s32[16]{0:T(128)S(1)}, /*index=5*/s32[]...) while((s32[]{:T(128)}, f32[4,512]{1,0:T(4,128)S(1)}, ...), condition=%wide.region_10.11_spmd.clone, body=%wide.region_3.10_spmd.clone.sunk | while | flops 551332864 | bytes 27935672 | solution.py:140
  306.0 6.3 %conditional.3 = ((f32[4,512]{1,0:T(4,128)S(1)}, f32[4,512]{1,0:T(4,128)S(1)}, f32[4,512,128]{2,1,0:T(8,128)})) conditional(s32[]{:T(128)} %convert_element_type.117, (f32[4,512]{1,0:T(4,128)S(1)}, f32[4,512]{1,0:T(4,128)S(1)}, f32[4,512,128]{2,1,0:T(8,128)}) %tuple.78, (s32[512]{0:T(512)S(1)}, s32[128]{0:T(128)S(1)}, s32[]{:T(128)}, ...), branch_computations={%region_6.6_spmd, %region_7.9_spmd} | conditional | flops 551292928 | bytes 27925118 | solution.py:138
  309.6 1.8 fusion.8
  314.4 6.3 %conditional.3 = ((f32[4,512]{1,0:T(4,128)S(1)}, f32[4,512]{1,0:T(4,128)S(1)}, f32[4,512,128]{2,1,0:T(8,128)})) conditional(s32[]{:T(128)} %convert_element_type.117, (f32[4,512]{1,0:T(4,128)S(1)}, f32[4,512]{1,0:T(4,128)S(1)}, f32[4,512,128]{2,1,0:T(8,128)}) %tuple.78, (s32[512]{0:T(512)S(1)}, s32[128]{0:T(128)S(1)}, s32[]{:T(128)}, ...), branch_computations={%region_6.6_spmd, %region_7.9_spmd} | conditional | flops 551292928 | bytes 27925118 | solution.py:138
  318.0 1.8 fusion.8
  322.9 6.3 %conditional.3 = ((f32[4,512]{1,0:T(4,128)S(1)}, f32[4,512]{1,0:T(4,128)S(1)}, f32[4,512,128]{2,1,0:T(8,128)})) conditional(s32[]{:T(128)} %convert_element_type.117, (f32[4,512]{1,0:T(4,128)S(1)}, f32[4,512]{1,0:T(4,128)S(1)}, f32[4,512,128]{2,1,0:T(8,128)}) %tuple.78, (s32[512]{0:T(512)S(1)}, s32[128]{0:T(128)S(1)}, s32[]{:T(128)}, ...), branch_computations={%region_6.6_spmd, %region_7.9_spmd} | conditional | flops 551292928 | bytes 27925118 | solution.py:138
  326.4 1.8 fusion.8
  331.3 6.3 %conditional.3 = ((f32[4,512]{1,0:T(4,128)S(1)}, f32[4,512]{1,0:T(4,128)S(1)}, f32[4,512,128]{2,1,0:T(8,128)})) conditional(s32[]{:T(128)} %convert_element_type.117, (f32[4,512]{1,0:T(4,128)S(1)}, f32[4,512]{1,0:T(4,128)S(1)}, f32[4,512,128]{2,1,0:T(8,128)}) %tuple.78, (s32[512]{0:T(512)S(1)}, s32[128]{0:T(128)S(1)}, s32[]{:T(128)}, ...), branch_computations={%region_6.6_spmd, %region_7.9_spmd} | conditional | flops 551292928 | bytes 27925118 | solution.py:138
  339.4 84.1 %all-gather.15.cloned.1.call-done = bf16[2048,4096]{1,0:T(8,128)(2,1)} async-done(((bf16[2048,256]{1,0:T(8,128)(2,1)}), bf16[2048,4096]{1,0:T(8,128)(2,1)}) %all-gather.15.cloned.1.call-update) | async-done | bytes 16777232 | tf_op jit(solution)/shard_map/all_gather | solution.py:149
  423.5 9.2 %convolution_convert_fusion = bf16[128,4096]{1,0:T(8,128)(2,1)} fusion(bf16[128,2048]{0,1:T(8,128)(2,1)S(1)} %bitcast.51, bf16[2048,4096]{1,0:T(8,128)(2,1)} %all-gather.15.cloned.1.call-done), kind=kOutput, calls=%fused_computation.31 | convolution fusion | flops 2148007936 | bytes 18350080 | tf_op jit(solution)/shard_map/dot_general | solution.py:147
  432.8 18.7 %reduce-scatter.2.cloned.1.call-done = bf16[128,2048]{1,0:T(8,128)(2,1)} async-done(((bf16[128,4096]{1,0:T(8,128)(2,1)}), bf16[128,2048]{1,0:T(8,128)(2,1)}) %reduce-scatter.2.cloned.1.call-update) | async-done | bytes 524304 | tf_op jit(solution)/shard_map/reduce_scatter | solution.py:152
  452.7 4.9 %psum.7 = f32[128]{0:T(128)S(1)} all-reduce(f32[128]{0:T(128)S(1)} %multiply_reduce_fusion), channel_id=1, replica_groups=mesh['seq'=16,'tp'=2] {'tp'}, use_global_device_ids=true, to_apply=%region_13.14 | all-reduce | flops 128 | bytes 1024 | tf_op jit(solution)/shard_map/psum | solution.py:157
  457.7 2.0 multiply_convert_fusion
  (113 shorter events, 36.2 us)
Async XLA Ops:
  7.2 26.4 %all-gather.7.cloned.1.call-start = ((), (), s32[]{:S(2)}) async-start(), calls=%async_computation.1 | async-start | bytes 1572864 | tf_op jit(solution)/shard_map/all_gather | solution.py:50
  7.9 102.8 %all-gather.9.cloned.1.call-start = ((), (), s32[]{:S(2)}) async-start(), calls=%async_computation.2 | async-start | bytes 8912896 | tf_op jit(solution)/shard_map/all_gather | solution.py:68
  9.9 156.5 %all-gather.11.cloned.1.call-start = ((), (), s32[]{:S(2)}) async-start(), calls=%async_computation.3 | async-start | bytes 4456448 | tf_op jit(solution)/shard_map/all_gather | solution.py:97
  115.8 3.5 copy-start.5
  117.2 176.1 %all-gather.13.cloned.1.call-start = ((), (), s32[]{:S(2)}) async-start(), calls=%async_computation.4 | async-start | bytes 17825792 | tf_op jit(solution)/shard_map/all_gather | solution.py:61
  117.8 305.7 %all-gather.15.cloned.1.call-start = ((), (), s32[]{:S(2)}) async-start(), calls=%async_computation.5 | async-start | bytes 17825792 | tf_op jit(solution)/shard_map/all_gather | solution.py:149
  118.4 333.1 %reduce-scatter.2.cloned.1.call-start = ((), (), s32[]{:S(2)}) async-start(), calls=%async_computation.6 | async-start | bytes 1572864 | tf_op jit(solution)/shard_map/reduce_scatter | solution.py:152
  170.8 122.6 %copy-start = (bf16[128,4096]{1,0:T(8,128)(2,1)S(1)}, bf16[128,4096]{1,0:T(8,128)(2,1)}, u32[]{:S(2)}) copy-start(bf16[128,4096]{1,0:T(8,128)(2,1)} %all-gather.7.cloned.1.call-done) | copy-start | bytes 3145732
  301.7 2.2 copy-start.4
  307.4 2.1 copy-start.2
  311.3 1.0 copy-start.3
  315.8 2.1 copy-start.2
  319.8 1.0 copy-start.3
  324.2 2.1 copy-start.2
  328.2 1.0 copy-start.3
  332.7 2.1 copy-start.2
  336.6 1.0 copy-start.3
  423.5 9.2 %copy-start.6 = (bf16[2048]{0:T(1024)(128)(2,1)S(1)}, bf16[2048]{0:T(1024)(128)(2,1)}, u32[]{:S(2)}) copy-start(bf16[2048]{0:T(1024)(128)(2,1)} %param.21) | copy-start | bytes 12292
  423.5 27.9 %copy-start.1 = (bf16[128,2048]{1,0:T(8,128)(2,1)S(1)}, bf16[128,2048]{1,0:T(8,128)(2,1)}, u32[]{:S(2)}) copy-start(bf16[128,2048]{1,0:T(8,128)(2,1)} %param.13) | copy-start | bytes 1572868
Sparse Core Ops, SparseCore 0:
  9.5 23.9 all-gather.6
  36.3 74.3 all-gather.8
  117.3 48.9 all-gather.10
  168.3 124.9 all-gather.12
  295.3 128.1 all-gather.14
  432.9 18.5 reduce-scatter.1
